TPU v7x, 64 devices: a 2x2x8 block of a 4x4x8 slice. The times are simulated.
64 devices in a mesh: rep: 8 (over x, y, core), dp: 8 (over z).
Axes of the slice: x: 2, y: 2, z: 8, core: 2. Of those that a mesh axis runs over, the one named last changes fastest.
The devices are a block of a 4x4x8 slice.
Arguments:
- g_w_gate: bfloat16 [64, 2, 896, 2560], P(('rep', 'dp')), parts along dimension 0
- g_w_up: bfloat16 [64, 2, 896, 2560], P(('rep', 'dp')), parts along dimension 0
- g_w_down: bfloat16 [64, 2, 2560, 896], P(('rep', 'dp')), parts along dimension 0
- w_gate: bfloat16 [2, 896, 2560], replicated
- w_up: bfloat16 [2, 896, 2560], replicated
- w_down: bfloat16 [2, 2560, 896], replicated
- m_w_gate: float32 [2, 896, 2560], P(None, 'dp')
- m_w_up: float32 [2, 896, 2560], P(None, 'dp')
- m_w_down: float32 [2, 2560, 896], P(None, 'dp')
- v_w_gate: float32 [2, 896, 2560], P(None, 'dp')
- v_w_up: float32 [2, 896, 2560], P(None, 'dp')
- v_w_down: float32 [2, 2560, 896], P(None, 'dp')
Outputs:
- output 1: bfloat16 [16, 896, 2560], P('rep'), parts along dimension 0
- output 2: bfloat16 [16, 896, 2560], P('rep'), parts along dimension 0
- output 3: bfloat16 [16, 2560, 896], P('rep'), parts along dimension 0
- output 4: float32 [16, 896, 2560], P('rep', 'dp'), parts along dimension 0
- output 5: float32 [16, 896, 2560], P('rep', 'dp'), parts along dimension 0
- output 6: float32 [16, 2560, 896], P('rep', 'dp'), parts along dimension 0
- output 7: float32 [16, 896, 2560], P('rep', 'dp'), parts along dimension 0
- output 8: float32 [16, 896, 2560], P('rep', 'dp'), parts along dimension 0
- output 9: float32 [16, 2560, 896], P('rep', 'dp'), parts along dimension 0
There are 8 independent parts. A program takes and returns all parts, laid end to end along the dimension named above; an argument that names none is the same for every part.
All inputs are finite; a program needn't handle non-finite values.
Results may differ from a plain program's by a relative error of at most 0.022.
Values are sent between devices in bfloat16 or wider.
A program may use at most 768 MiB of HBM per device.

v0:
```python
import jax
import jax.numpy as jnp
from jax import lax
from jax.sharding import PartitionSpec as P


def adamw(w, m, v, g):
    m = 0.9 * m + 0.1 * g
    v = 0.95 * v + 0.05 * g * g
    step = m * lax.rsqrt(v + 1e-8) + 0.1 * w
    return (w - 0.02 * step).astype(jnp.bfloat16), m, v


def solution(mesh):
    def step(*arrays):
        terms, weights, m, v = (arrays[i : i + 3] for i in (0, 3, 6, 9))
        gradients = [lax.psum_scatter(t[0], "dp", scatter_dimension=1, tiled=True).astype(jnp.float32) for t in terms]
        me = lax.axis_index("dp")
        own = [lax.dynamic_slice_in_dim(w, me * one.shape[1], one.shape[1], 1).astype(jnp.float32) for w, one in zip(weights, m, strict=True)]
        new = [adamw(w, m, v, g) for w, m, v, g in zip(own, m, v, gradients, strict=True)]
        whole = [lax.all_gather(one[0], "dp", axis=1, tiled=True) for one in new]
        return (*whole, *(one[1] for one in new), *(one[2] for one in new))

    all_of, cut = P(None, None, None), P(None, "dp", None)
    return jax.shard_map(
        step,
        mesh=mesh,
        in_specs=(P(("rep", "dp"), None, None, None),) * 3 + (all_of,) * 3 + (cut,) * 6,
        out_specs=(P("rep", None, None),) * 3 + (P("rep", "dp", None),) * 6,
        check_vma=False,
    )
```

profile of v0, /device:TPU:22, one launch (start us, length us, event | category | flops | bytes accessed | tf_op | source)
XLA Modules:
  0.0 640.1 jit_solution(12494109477832534822)
XLA Ops:
  7.2 0.1 reduce-scatter.8.cloned.1.call-start
  7.3 0.7 reduce-scatter.8.cloned.1.call-update
  8.0 0.1 reduce-scatter.6.cloned.1.call-start
  8.1 0.7 reduce-scatter.6.cloned.1.call-update
  8.8 0.1 reduce-scatter.4.cloned.1.call-start
  8.9 0.0 copy-start
  8.9 0.7 reduce-scatter.4.cloned.1.call-update
  9.6 0.1 all-gather.8.cloned.1.call-start
  9.7 103.6 %reduce-scatter.8.cloned.1.call-done = bf16[2,320,896]{2,1,0:T(8,128)(2,1)} async-done(((bf16[2,2560,896]{2,1,0:T(8,128)(2,1)}), bf16[2,320,896]{2,1,0:T(8,128)(2,1)}) %reduce-scatter.8.cloned.1.call-update) | async-done | bytes 1146896 | tf_op jit(solution)/shard_map/reduce_scatter | solution.py:17
  113.2 0.0 copy-done
  113.2 5.5 fusion.10
  118.8 0.1 all-gather.8.cloned.1.call-update
  118.8 0.1 all-gather.6.cloned.1.call-start
  118.9 94.4 %reduce-scatter.6.cloned.1.call-done = bf16[2,112,2560]{2,1,0:T(8,128)(2,1)} async-done(((bf16[2,896,2560]{2,1,0:T(8,128)(2,1)}), bf16[2,112,2560]{2,1,0:T(8,128)(2,1)}) %reduce-scatter.6.cloned.1.call-update) | async-done | bytes 1146896 | tf_op jit(solution)/shard_map/reduce_scatter | solution.py:17
  213.3 0.0 copy-start.1
  213.3 6.3 fusion.6
  219.7 0.1 all-gather.6.cloned.1.call-update
  219.7 0.1 all-gather.4.cloned.1.call-start
  219.8 93.6 %reduce-scatter.4.cloned.1.call-done = bf16[2,112,2560]{2,1,0:T(8,128)(2,1)} async-done(((bf16[2,896,2560]{2,1,0:T(8,128)(2,1)}), bf16[2,112,2560]{2,1,0:T(8,128)(2,1)}) %reduce-scatter.4.cloned.1.call-update) | async-done | bytes 1146896 | tf_op jit(solution)/shard_map/reduce_scatter | solution.py:17
  313.4 0.0 copy-done.1
  313.4 5.5 fusion.2
  319.0 0.1 all-gather.4.cloned.1.call-update
  319.0 93.2 %all-gather.8.cloned.1.call-done = bf16[2,2560,896]{2,1,0:T(8,128)(2,1)} async-done(((bf16[2,320,896]{2,1,0:T(8,128)(2,1)}), bf16[2,2560,896]{2,1,0:T(8,128)(2,1)}) %all-gather.8.cloned.1.call-update) | async-done | bytes 9175056 | tf_op jit(solution)/shard_map/all_gather | solution.py:21
  412.2 98.7 %all-gather.6.cloned.1.call-done = bf16[2,896,2560]{2,1,0:T(8,128)(2,1)} async-done(((bf16[2,112,2560]{2,1,0:T(8,128)(2,1)}), bf16[2,896,2560]{2,1,0:T(8,128)(2,1)}) %all-gather.6.cloned.1.call-update) | async-done | bytes 9175056 | tf_op jit(solution)/shard_map/all_gather | solution.py:21
  510.9 98.7 %all-gather.4.cloned.1.call-done = bf16[2,896,2560]{2,1,0:T(8,128)(2,1)} async-done(((bf16[2,112,2560]{2,1,0:T(8,128)(2,1)}), bf16[2,896,2560]{2,1,0:T(8,128)(2,1)}) %all-gather.4.cloned.1.call-update) | async-done | bytes 9175056 | tf_op jit(solution)/shard_map/all_gather | solution.py:21
  609.6 7.8 %copy.24 = bf16[2,896,2560]{2,1,0:T(8,128)(2,1)} copy(bf16[2,896,2560]{2,1,0:T(8,128)(2,1)} %all-gather.4.cloned.1.call-done) | data formatting | bytes 18350080
  617.4 7.8 %copy.25 = bf16[2,896,2560]{2,1,0:T(8,128)(2,1)} copy(bf16[2,896,2560]{2,1,0:T(8,128)(2,1)} %all-gather.6.cloned.1.call-done) | data formatting | bytes 18350080
  625.3 8.0 %copy.26 = bf16[2,2560,896]{2,1,0:T(8,128)(2,1)} copy(bf16[2,2560,896]{2,1,0:T(8,128)(2,1)} %all-gather.8.cloned.1.call-done) | data formatting | bytes 18350080
Async XLA Ops:
  7.2 106.0 %reduce-scatter.8.cloned.1.call-start = ((), (), s32[]{:S(2)}) async-start(), calls=%async_computation.7 | async-start | bytes 10321920 | tf_op jit(solution)/shard_map/reduce_scatter | solution.py:17
  8.0 205.3 %reduce-scatter.6.cloned.1.call-start = ((), (), s32[]{:S(2)}) async-start(), calls=%async_computation.5 | async-start | bytes 10321920 | tf_op jit(solution)/shard_map/reduce_scatter | solution.py:17
  8.8 304.6 %reduce-scatter.4.cloned.1.call-start = ((), (), s32[]{:S(2)}) async-start(), calls=%async_computation.3 | async-start | bytes 10321920 | tf_op jit(solution)/shard_map/reduce_scatter | solution.py:17
  8.9 104.4 %copy-start = (f32[2,320,896]{2,1,0:T(8,128)S(1)}, f32[2,320,896]{2,1,0:T(8,128)}, u32[]{:S(2)}) copy-start(f32[2,320,896]{2,1,0:T(8,128)} %param.23) | copy-start | bytes 6881284
  9.6 402.6 %all-gather.8.cloned.1.call-start = ((), (), s32[]{:S(2)}) async-start(), calls=%async_computation.8 | async-start | bytes 10321920 | tf_op jit(solution)/shard_map/all_gather | solution.py:21
  118.8 392.0 %all-gather.6.cloned.1.call-start = ((), (), s32[]{:S(2)}) async-start(), calls=%async_computation.6 | async-start | bytes 10321920 | tf_op jit(solution)/shard_map/all_gather | solution.py:21
  213.3 100.1 %copy-start.1 = (f32[2,112,2560]{2,1,0:T(8,128)S(1)}, f32[2,112,2560]{2,1,0:T(8,128)}, u32[]{:S(2)}) copy-start(f32[2,112,2560]{2,1,0:T(8,128)} %param.21) | copy-start | bytes 6881284
  219.7 389.8 %all-gather.4.cloned.1.call-start = ((), (), s32[]{:S(2)}) async-start(), calls=%async_computation.4 | async-start | bytes 10321920 | tf_op jit(solution)/shard_map/all_gather | solution.py:21
Sparse Core Ops, SparseCore 0:
  10.4 102.8 reduce-scatter.7
  115.6 97.6 reduce-scatter.5
  215.7 97.6 reduce-scatter.3
  315.5 96.6 all-gather.7
  414.2 96.6 all-gather.5
  512.9 96.6 all-gather.3
where the time goes:
time: 641 us; the launch traced here: 640 us
  waiting for transfers between devices  585 us (91%)
  local copies, waits for them, and re-layouts  23.7 us (4%)
  other arithmetic  17.4 us (3%)
  between operations  14.2 us (2%)
    reduce_scatter x3, waiting for transfers between devices, step(): lax.psum_scatter(t[0], 'dp', scatter_dimension=1, tiled=True)  292 us
    all_gather x3, waiting for transfers between devices, step(): whole = [lax.all_gather(one[0], 'dp', axis=1, tiled=True) for one in new]  291 us
    unnamed x7, local copies, waits for them, and re-layouts  23.7 us
    convert_element_type x3, other arithmetic, adamw(): return ((w - 0.02 * step).astype(jnp.bfloat16), m, v)  17.4 us
  transfers between devices with their start and end apart: 6, of which 6 were waited for; matrix products, arithmetic and copies ran while one was open for 3% of the time, Pallas kernels for 0%

commit v1 on v0

v1 whole, which is shorter than its diff:
```python
import functools

import jax
import jax.numpy as jnp
from jax import lax
from jax.experimental import pallas as pl
from jax.experimental.pallas import tpu as pltpu
from jax.sharding import PartitionSpec as P

MESH = pl.DeviceIdType.MESH
SLOTS = 3
F32, BF16 = jnp.float32, jnp.bfloat16


def tiles(rows, cols, wide):
    step = cols
    while step > wide and step % 256 == 0:
        step //= 2
    return 16, step


def kernel(n, *refs):
    terms, weights, old_m, old_v = (refs[i : i + 3] for i in (0, 3, 6, 9))
    whole, new_m, new_v = (refs[i : i + 3] for i in (12, 15, 18))
    slots, own, held = (refs[i : i + 3] for i in (21, 24, 27))
    sum_send, sum_recv, out_send, out_recv, own_sem, held_sem, m_sem, v_sem, free = refs[30:]
    me = lax.axis_index("dp")
    right, left = lax.rem(me + 1, n), lax.rem(me + n - 1, n)
    ahead, behind, way = (right, left), (left, right), (1, -1)
    units = [(w, d) for w in range(3) for d in range(2)]
    rows = [m.shape[1] for m in new_m]

    def index(d, hops):
        return lax.rem(me - way[d] * hops + 2 * n, n)

    def block(w, owner):
        return pl.ds(pl.multiple_of(owner * rows[w], rows[w]), rows[w])

    def load_own(w, d, hops):
        return pltpu.make_async_copy(terms[w].at[0, d, block(w, index(d, hops))], own[w].at[d], own_sem.at[w, d])

    def load_held(w, d):
        return pltpu.make_async_copy(weights[w].at[d, block(w, me)], held[w].at[d], held_sem.at[w, d])

    def load_m(w, d):
        return pltpu.make_async_copy(old_m[w].at[d], new_m[w].at[d], m_sem.at[w, d])

    def load_v(w, d):
        return pltpu.make_async_copy(old_v[w].at[d], new_v[w].at[d], v_sem.at[w, d])

    def pass_sum(w, d, step, source):
        slot = lax.rem(step, SLOTS)
        return pltpu.make_async_remote_copy(
            src_ref=source,
            dst_ref=slots[w].at[d, slot],
            send_sem=sum_send.at[w, d],
            recv_sem=sum_recv.at[w, d, slot],
            device_id={"dp": ahead[d]},
            device_id_type=MESH,
        )

    def pass_new(w, d, step):
        piece = whole[w].at[d, block(w, index(d, step))]
        return pltpu.make_async_remote_copy(
            src_ref=piece,
            dst_ref=piece,
            send_sem=out_send.at[w, d],
            recv_sem=out_recv.at[w, d, step],
            device_id={"dp": ahead[d]},
            device_id_type=MESH,
        )

    def slot_of(w, d, step):
        return slots[w].at[d, lax.rem(step, SLOTS)]

    def over(w, wide, body):
        high, across = tiles(rows[w], whole[w].shape[2], wide)

        @pl.loop(0, rows[w] // high)
        def _(i):
            for c in range(0, whole[w].shape[2], across):
                body(pl.ds(pl.multiple_of(i * high, high), high), pl.ds(c, across))

    for w, d in units:
        load_own(w, d, 2).start()
    barrier = pltpu.get_barrier_semaphore()
    for other in (left, right):
        pl.semaphore_signal(barrier, inc=1, device_id={"dp": other}, device_id_type=MESH)
    pl.semaphore_wait(barrier, 2)

    for w, d in units:
        pass_sum(w, d, 0, terms[w].at[0, d, block(w, index(d, 1))]).start()
    for w, d in units:
        load_held(w, d).start()
        load_m(w, d).start()
        load_v(w, d).start()

    @pl.loop(1, n - 1)
    def _(step):
        for w in range(3):
            for d in range(2):
                pass_sum(w, d, step - 1, slot_of(w, d, step - 1)).wait_recv()
                pass_sum(w, d, step - 1, slot_of(w, d, step - 1)).wait_send()
                load_own(w, d, 0).wait()

                @pl.when((step >= 2) & (step < n - 2))
                def _():
                    pl.semaphore_signal(free.at[w, d], inc=1, device_id={"dp": behind[d]}, device_id_type=MESH)

            for d in range(2):
                so_far = slot_of(w, d, step - 1)

                def add(r, c, so_far=so_far, d=d):
                    so_far[r, c] = (so_far[r, c].astype(F32) + own[w][d, r, c].astype(F32)).astype(BF16)

                over(w, 1280, add)
            for d in range(2):
                load_own(w, d, step + 2).start()

                @pl.when(step >= SLOTS)
                def _():
                    pl.semaphore_wait(free.at[w, d], 1)

            for d in range(2):
                pass_sum(w, d, step, slot_of(w, d, step - 1)).start()

    for w in range(3):
        for d in range(2):
            pass_sum(w, d, n - 2, slot_of(w, d, n - 2)).wait_recv()
            pass_sum(w, d, n - 2, slot_of(w, d, n - 2)).wait_send()
            load_own(w, d, 0).wait()
            load_held(w, d).wait()
            load_m(w, d).wait()
            load_v(w, d).wait()
        for d in range(2):
            so_far = slot_of(w, d, n - 2)

            def adamw(r, c, so_far=so_far, d=d):
                g = (so_far[r, c].astype(F32) + own[w][d, r, c].astype(F32)).astype(BF16).astype(F32)
                m = 0.9 * new_m[w][d, r, c] + 0.1 * g
                v = 0.95 * new_v[w][d, r, c] + 0.05 * g * g
                step = m * lax.rsqrt(v + 1e-8) + 0.1 * held[w][d, r, c].astype(F32)
                new_m[w][d, r, c] = m
                new_v[w][d, r, c] = v
                mine = pl.multiple_of(me * rows[w], 16) + r.start
                whole[w][d, pl.ds(pl.multiple_of(mine, 16), 16), c] = (held[w][d, r, c].astype(F32) - 0.02 * step).astype(BF16)

            over(w, 640, adamw)
        for d in range(2):
            pass_new(w, d, 0).start()

    @pl.loop(1, n - 1)
    def _(step):
        for w, d in units:
            pass_new(w, d, step - 1).wait_recv()
            pass_new(w, d, step - 1).wait_send()
            pass_new(w, d, step).start()

    for w, d in units:
        pass_new(w, d, n - 2).wait()


def put_out(*refs):
    half = len(refs) // 2
    arrays, results, sem = refs[:half], refs[half : 2 * half], refs[-1]
    copies = [pltpu.make_async_copy(a.at[d], r.at[d], sem.at[i, d]) for i, (a, r) in enumerate(zip(arrays, results, strict=True)) for d in range(2)]
    for one in copies:
        one.start()
    for one in copies:
        one.wait()


def solution(mesh):
    n = mesh.shape["dp"]

    def step(*arrays):
        terms, weights, m, v = (arrays[i : i + 3] for i in (0, 3, 6, 9))
        shard = [one.shape for one in m]
        anywhere, vmem = pl.BlockSpec(memory_space=pl.ANY), pl.BlockSpec(memory_space=pltpu.VMEM)
        dma = pltpu.SemaphoreType.DMA
        inputs = (pltpu.with_memory_space_constraint(x, pltpu.HBM) for x in (*terms, *weights, *m, *v))
        made = pl.pallas_call(
            functools.partial(kernel, n),
            out_shape=tuple(pltpu.VMEM(x.shape, x.dtype) for x in (*weights, *m, *v)),
            in_specs=[pl.BlockSpec(memory_space=pltpu.HBM)] * 12,
            out_specs=(vmem,) * 9,
            scratch_shapes=[
                *(pltpu.VMEM((2, SLOTS, *s[1:]), BF16) for s in shard),
                *(pltpu.VMEM(s, BF16) for s in shard),
                *(pltpu.VMEM(s, BF16) for s in shard),
                dma((3, 2)),
                dma((3, 2, SLOTS)),
                dma((3, 2)),
                dma((3, 2, n - 1)),
                dma((3, 2)),
                dma((3, 2)),
                dma((3, 2)),
                dma((3, 2)),
                pltpu.SemaphoreType.REGULAR((3, 2)),
            ],
            compiler_params=pltpu.CompilerParams(collective_id=0, has_side_effects=True, vmem_limit_bytes=20 * 2**20),
            name="step",
        )(*inputs)
        return pl.pallas_call(
            put_out,
            out_shape=tuple(jax.ShapeDtypeStruct(x.shape, x.dtype) for x in (*weights, *m, *v)),
            in_specs=[vmem] * 9,
            out_specs=(anywhere,) * 9,
            scratch_shapes=[dma((9, 2))],
            compiler_params=pltpu.CompilerParams(has_side_effects=True, vmem_limit_bytes=20 * 2**20),
            name="put_out",
        )(*(pltpu.with_memory_space_constraint(x, pltpu.VMEM) for x in made))

    all_of, cut = P(None, None, None), P(None, "dp", None)
    return jax.shard_map(
        step,
        mesh=mesh,
        in_specs=(P(("rep", "dp"), None, None, None),) * 3 + (all_of,) * 3 + (cut,) * 6,
        out_specs=(P("rep", None, None),) * 3 + (P("rep", "dp", None),) * 6,
        check_vma=False,
    )
```

time: 641 us -> 540 us (0.84)
  waiting for transfers between devices: 585 us -> 0 us
  Pallas kernels: 0 us -> 539 us
  local copies, waits for them, and re-layouts: 23.7 us -> 0 us
  other arithmetic: 17.4 us -> 0 us
  between operations: 14.2 us -> 0.65 us
    pallas_call x0 -> x2, Pallas kernels: none -> 539 us  [the longest x1 526 us: step(): pl.pallas_call(functools.partial(kernel, n), out_shape=tuple((pltpu.VMEM(...]
    reduce_scatter x3 -> x0, waiting for transfers between devices: 292 us -> none  [step(): lax.psum_scatter(t[0], 'dp', scatter_dimension=1, tiled=True)]
    all_gather x3 -> x0, waiting for transfers between devices: 291 us -> none  [step(): whole = [lax.all_gather(one[0], 'dp', axis=1, tiled=True) for one in new]]
    unnamed x7 -> x0, local copies, waits for them, and re-layouts: 23.7 us -> none
    convert_element_type x3 -> x0, other arithmetic: 17.4 us -> none  [adamw(): return ((w - 0.02 * step).astype(jnp.bfloat16), m, v)]
  transfers between devices with their start and end apart: 6 -> 0, of which waited for: 6 -> 0; matrix products, arithmetic and copies ran while one was open for 3% -> 0% of each run, Pallas kernels for 0% -> 0%
where the time goes in v1:
time: 540 us
  Pallas kernels  539 us (100%)
    pallas_call x1, Pallas kernels, step(): pl.pallas_call(functools.partial(kernel, n), out_shape=tuple((pltpu.VMEM(...  526 us
    pallas_call x1, Pallas kernels, step(): pl.pallas_call(put_out, out_shape=tuple((jax.ShapeDtypeStruct(x.shape, x....  13.4 us

profile of v1, /device:TPU:22, one launch (start us, length us, event | category | flops | bytes accessed | tf_op | source)
XLA Modules:
  0.0 539.7 jit_solution(16558815880405701395)
XLA Ops:
  0.6 525.7 %step.1 = (bf16[2,896,2560]{2,1,0:T(8,128)(2,1)S(1)}, bf16[2,896,2560]{2,1,0:T(8,128)(2,1)S(1)}, bf16[2,2560,896]{2,1,0:T(8,128)(2,1)S(1)}, f32[2,112,2560]{2,1,...) custom-call(bf16[1,2,896,2560]{3,2,1,0:T(8,128)(2,1)} %refs_0_.1, ...), custom_call_target="tpu_custom_call" | custom-call | tf_op jit(solution)/shard_map/step/pallas_call | solution.py:182
  526.4 13.4 %put_out.1 = (bf16[2,896,2560]{2,1,0:T(8,128)(2,1)}, bf16[2,896,2560]{2,1,0:T(8,128)(2,1)}, bf16[2,2560,896]{2,1,0:T(8,128)(2,1)}, f32[2,112,2560]{2,1,0:T(8,128...) custom-call(bf16[2,896,2560]{2,1,0:T(8,128)(2,1)S(1)} %get-tuple-ele, ...), custom_call_target="tpu_custom_call" | custom-call | tf_op jit(solution)/shard_map/put_out/pallas_call | solution.py:204

commit v2 on v1

--- a/solution.py
+++ b/solution.py
@@ -9,6 +9,7 @@
 
 MESH = pl.DeviceIdType.MESH
 SLOTS = 3
+COST = 100_000_000
 F32, BF16 = jnp.float32, jnp.bfloat16
 
 
@@ -22,8 +23,9 @@
 def kernel(n, *refs):
     terms, weights, old_m, old_v = (refs[i : i + 3] for i in (0, 3, 6, 9))
     whole, new_m, new_v = (refs[i : i + 3] for i in (12, 15, 18))
-    slots, own, held = (refs[i : i + 3] for i in (21, 24, 27))
-    sum_send, sum_recv, out_send, out_recv, own_sem, held_sem, m_sem, v_sem, free = refs[30:]
+    last = refs[21:23]
+    slots, own, held = (refs[i : i + 3] for i in (23, 26, 29))
+    sum_send, sum_recv, out_send, out_recv, own_sem, held_sem, m_sem, v_sem, free = refs[32:]
     me = lax.axis_index("dp")
     right, left = lax.rem(me + 1, n), lax.rem(me + n - 1, n)
     ahead, behind, way = (right, left), (left, right), (1, -1)
@@ -61,9 +63,10 @@
 
     def pass_new(w, d, step):
         piece = whole[w].at[d, block(w, index(d, step))]
+        lands = last[d] if w == 2 and isinstance(step, int) and step == n - 3 else piece
         return pltpu.make_async_remote_copy(
             src_ref=piece,
-            dst_ref=piece,
+            dst_ref=lands,
             send_sem=out_send.at[w, d],
             recv_sem=out_recv.at[w, d, step],
             device_id={"dp": ahead[d]},
@@ -149,21 +152,56 @@
         for d in range(2):
             pass_new(w, d, 0).start()
 
-    @pl.loop(1, n - 1)
+    def forward(w, d, step):
+        pass_new(w, d, step - 1).wait_recv()
+        pass_new(w, d, step - 1).wait_send()
+        pass_new(w, d, step).start()
+
+    @pl.loop(1, n - 3)
     def _(step):
         for w, d in units:
-            pass_new(w, d, step - 1).wait_recv()
-            pass_new(w, d, step - 1).wait_send()
-            pass_new(w, d, step).start()
-
-    for w, d in units:
-        pass_new(w, d, n - 2).wait()
-
-
-def put_out(*refs):
-    half = len(refs) // 2
-    arrays, results, sem = refs[:half], refs[half : 2 * half], refs[-1]
-    copies = [pltpu.make_async_copy(a.at[d], r.at[d], sem.at[i, d]) for i, (a, r) in enumerate(zip(arrays, results, strict=True)) for d in range(2)]
+            forward(w, d, step)
+
+    for w, d in units:
+        forward(w, d, n - 3)
+    for w, d in units:
+        if w < 2:
+            forward(w, d, n - 2)
+        else:
+            pass_new(w, d, n - 3).wait()
+    for w, d in units:
+        if w < 2:
+            pass_new(w, d, n - 2).wait()
+
+
+def put_out(n, *refs):
+    arrays, last, results, sem, block_sem = refs[:9], refs[9:11], refs[11:20], refs[20], refs[21]
+    me = lax.axis_index("dp")
+    rows = last[0].shape[0]
+    copies = []
+    for i, (a, r) in enumerate(zip(arrays, results, strict=True)):
+        for d in range(2):
+            if i == 2:
+                for hops in range(n - 1):
+                    owner = lax.rem(me + (n - hops if d == 0 else hops), n)
+                    piece = pl.ds(pl.multiple_of(owner * rows, rows), rows)
+                    source = last[d] if hops == n - 2 else a.at[d, piece]
+                    copies.append(pltpu.make_async_copy(source, r.at[d, piece], block_sem.at[d, hops]))
+            else:
+                copies.append(pltpu.make_async_copy(a.at[d], r.at[d], sem.at[i, d]))
+    for one in copies:
+        one.start()
+    for one in copies:
+        one.wait()
+
+
+def put_last(n, so_far, from_left, from_right, result, sem):
+    me = lax.axis_index("dp")
+    rows = from_left.shape[0]
+    copies = []
+    for d, one in enumerate((from_left, from_right)):
+        owner = lax.rem(me + (1 if d == 0 else n - 1), n)
+        copies.append(pltpu.make_async_copy(one, result.at[d, pl.ds(pl.multiple_of(owner * rows, rows), rows)], sem.at[d]))
     for one in copies:
         one.start()
     for one in copies:
@@ -176,14 +214,14 @@
     def step(*arrays):
         terms, weights, m, v = (arrays[i : i + 3] for i in (0, 3, 6, 9))
         shard = [one.shape for one in m]
-        anywhere, vmem = pl.BlockSpec(memory_space=pl.ANY), pl.BlockSpec(memory_space=pltpu.VMEM)
+        hbm, vmem = pl.BlockSpec(memory_space=pltpu.HBM), pl.BlockSpec(memory_space=pltpu.VMEM)
         dma = pltpu.SemaphoreType.DMA
         inputs = (pltpu.with_memory_space_constraint(x, pltpu.HBM) for x in (*terms, *weights, *m, *v))
         made = pl.pallas_call(
             functools.partial(kernel, n),
-            out_shape=tuple(pltpu.VMEM(x.shape, x.dtype) for x in (*weights, *m, *v)),
-            in_specs=[pl.BlockSpec(memory_space=pltpu.HBM)] * 12,
-            out_specs=(vmem,) * 9,
+            out_shape=(*(pltpu.VMEM(x.shape, x.dtype) for x in (*weights, *m, *v)), *(pltpu.VMEM(shard[2][1:], BF16),) * 2),
+            in_specs=[hbm] * 12,
+            out_specs=(vmem,) * 11,
             scratch_shapes=[
                 *(pltpu.VMEM((2, SLOTS, *s[1:]), BF16) for s in shard),
                 *(pltpu.VMEM(s, BF16) for s in shard),
@@ -201,15 +239,29 @@
             compiler_params=pltpu.CompilerParams(collective_id=0, has_side_effects=True, vmem_limit_bytes=20 * 2**20),
             name="step",
         )(*inputs)
-        return pl.pallas_call(
-            put_out,
+        last_0, last_1 = made[9:]
+        last = [lax.ppermute(one, "dp", [(i, (i + way) % n) for i in range(n)]) for one, way in ((last_0, 1), (last_1, -1))]
+        out = pl.pallas_call(
+            functools.partial(put_out, n),
             out_shape=tuple(jax.ShapeDtypeStruct(x.shape, x.dtype) for x in (*weights, *m, *v)),
-            in_specs=[vmem] * 9,
-            out_specs=(anywhere,) * 9,
-            scratch_shapes=[dma((9, 2))],
+            in_specs=[vmem] * 11,
+            out_specs=(hbm,) * 9,
+            scratch_shapes=[dma((9, 2)), dma((2, n - 1))],
             compiler_params=pltpu.CompilerParams(has_side_effects=True, vmem_limit_bytes=20 * 2**20),
+            cost_estimate=pl.CostEstimate(flops=COST, bytes_accessed=80_000_000, transcendentals=0),
             name="put_out",
         )(*(pltpu.with_memory_space_constraint(x, pltpu.VMEM) for x in made))
+        down = pl.pallas_call(
+            functools.partial(put_last, n),
+            out_shape=jax.ShapeDtypeStruct(weights[2].shape, BF16),
+            in_specs=[hbm, vmem, vmem],
+            out_specs=hbm,
+            input_output_aliases={0: 0},
+            scratch_shapes=[dma((2,))],
+            compiler_params=pltpu.CompilerParams(has_side_effects=True, vmem_limit_bytes=20 * 2**20),
+            name="put_last",
+        )(pltpu.with_memory_space_constraint(out[2], pltpu.HBM), *(pltpu.with_memory_space_constraint(x, pltpu.VMEM) for x in last))
+        return (*out[:2], down, *out[3:])
 
     all_of, cut = P(None, None, None), P(None, "dp", None)
     return jax.shard_map(

time: 540 us -> 532 us (0.985)
  Pallas kernels: 539 us -> 528 us
    pallas_call x2 -> x3, Pallas kernels: 539 us -> 528 us  [the longest x1 513 us: step(): pl.pallas_call(functools.partial(kernel, n), out_shape=(*(pltpu.VMEM(x.sh...]
  transfers between devices with their start and end apart: 0 -> 2, of which waited for: 0 -> 0; matrix products, arithmetic and copies ran while one was open for 0% -> 0% of each run, Pallas kernels for 0% -> 2%
where the time goes in v2:
time: 532 us
  Pallas kernels  528 us (99%)
    pallas_call x1, Pallas kernels, step(): pl.pallas_call(functools.partial(kernel, n), out_shape=(*(pltpu.VMEM(x.sh...  513 us
    pallas_call x1, Pallas kernels, step(): pl.pallas_call(functools.partial(put_out, n), out_shape=tuple((jax.ShapeD...  13.1 us
  transfers between devices with their start and end apart: 2, of which 0 were waited for; matrix products, arithmetic and copies ran while one was open for 0% of the time, Pallas kernels for 2%

profile of v2, /device:TPU:22, one launch (start us, length us, event | category | flops | bytes accessed | tf_op | source)
XLA Modules:
  0.0 531.6 jit_solution(2253605611294009131)
XLA Ops:
  0.6 513.4 %step.1 = (bf16[2,896,2560]{2,1,0:T(8,128)(2,1)S(1)}, bf16[2,896,2560]{2,1,0:T(8,128)(2,1)S(1)}, bf16[2,2560,896]{2,1,0:T(8,128)(2,1)S(1)}, f32[2,112,2560]{2,1,...) custom-call(bf16[1,2,896,2560]{3,2,1,0:T(8,128)(2,1)} %refs_0_.1, ...), custom_call_target="tpu_custom_call" | custom-call | tf_op jit(solution)/shard_map/step/pallas_call | solution.py:220
  514.1 1.3 collective-permute-start
  515.4 2.0 collective-permute-start.1
  517.4 13.1 %put_out.1 = (bf16[2,896,2560]{2,1,0:T(8,128)(2,1)}, bf16[2,896,2560]{2,1,0:T(8,128)(2,1)}, bf16[2,2560,896]{2,1,0:T(8,128)(2,1)}, f32[2,112,2560]{2,1,0:T(8,128...) custom-call(bf16[2,896,2560]{2,1,0:T(8,128)(2,1)S(1)} %get-tuple-ele, ...), custom_call_target="tpu_custom_call" | custom-call | flops 100000000 | bytes 80000000 | tf_op jit(solution)/shard_map/put_out/pallas_call | solution.py:244
  530.5 0.0 collective-permute-done.from_left
  530.6 0.0 collective-permute-done.1.from_right
  530.6 1.0 put_last.1
Async XLA Ops:
  514.1 16.5 %collective-permute-start = (bf16[320,896]{1,0:T(8,128)(2,1)S(1)}, bf16[320,896]{1,0:T(8,128)(2,1)S(1)}, u32[]{:S(2)}, u32[]{:S(2)}) collective-permute-start(bf16[320,896]{1,0:T(8,128)(2,1)S(1)} %get-tuple-element.38.refs_9_), channel_id=1, source_target_pairs={{0,1},{1,2},{2,3},{3,4},{4,5},{5,6},{6,7},{7,0},{8,9},{9,10},{10,1... | collective-permute-start | bytes 1720328 | tf_op jit(solution)/shard_map/ppermute | solution.py:243
  515.4 15.2 %collective-permute-start.1 = (bf16[320,896]{1,0:T(8,128)(2,1)S(1)}, bf16[320,896]{1,0:T(8,128)(2,1)S(1)}, u32[]{:S(2)}, u32[]{:S(2)}) collective-permute-start(bf16[320,896]{1,0:T(8,128)(2,1)S(1)} %get-tuple-element.39.refs_10_), channel_id=1, source_target_pairs={{0,7},{1,0},{2,1},{3,2},{4,3},{5,4},{6,5},{7,6},{8,15},{9,8},{10,9... | collective-permute-start | bytes 1720328 | tf_op jit(solution)/shard_map/ppermute | solution.py:243

commit v3 on v2

--- a/solution.py
+++ b/solution.py
@@ -10,6 +10,7 @@
 MESH = pl.DeviceIdType.MESH
 SLOTS = 3
 COST = 100_000_000
+ROOM = 17 * 2**20
 F32, BF16 = jnp.float32, jnp.bfloat16
 
 
@@ -29,7 +30,8 @@
     me = lax.axis_index("dp")
     right, left = lax.rem(me + 1, n), lax.rem(me + n - 1, n)
     ahead, behind, way = (right, left), (left, right), (1, -1)
-    units = [(w, d) for w in range(3) for d in range(2)]
+    order = (2, 0, 1)
+    units = [(w, d) for w in order for d in range(2)]
     rows = [m.shape[1] for m in new_m]
 
     def index(d, hops):
@@ -63,7 +65,7 @@
 
     def pass_new(w, d, step):
         piece = whole[w].at[d, block(w, index(d, step))]
-        lands = last[d] if w == 2 and isinstance(step, int) and step == n - 3 else piece
+        lands = last[d].at[w] if w < 2 and isinstance(step, int) and step == n - 3 else piece
         return pltpu.make_async_remote_copy(
             src_ref=piece,
             dst_ref=lands,
@@ -91,16 +93,25 @@
         pl.semaphore_signal(barrier, inc=1, device_id={"dp": other}, device_id_type=MESH)
     pl.semaphore_wait(barrier, 2)
 
-    for w, d in units:
-        pass_sum(w, d, 0, terms[w].at[0, d, block(w, index(d, 1))]).start()
+    late = lax.rem(lax.axis_index("rep"), 2) == 0
     for w, d in units:
         load_held(w, d).start()
         load_m(w, d).start()
         load_v(w, d).start()
 
+    @pl.when(late)
+    def _():
+        for w, d in units:
+            load_held(w, d).wait()
+            load_m(w, d).wait()
+            load_v(w, d).wait()
+
+    for w, d in units:
+        pass_sum(w, d, 0, terms[w].at[0, d, block(w, index(d, 1))]).start()
+
     @pl.loop(1, n - 1)
     def _(step):
-        for w in range(3):
+        for w in order:
             for d in range(2):
                 pass_sum(w, d, step - 1, slot_of(w, d, step - 1)).wait_recv()
                 pass_sum(w, d, step - 1, slot_of(w, d, step - 1)).wait_send()
@@ -127,14 +138,18 @@
             for d in range(2):
                 pass_sum(w, d, step, slot_of(w, d, step - 1)).start()
 
-    for w in range(3):
+    for w in order:
         for d in range(2):
             pass_sum(w, d, n - 2, slot_of(w, d, n - 2)).wait_recv()
             pass_sum(w, d, n - 2, slot_of(w, d, n - 2)).wait_send()
             load_own(w, d, 0).wait()
-            load_held(w, d).wait()
-            load_m(w, d).wait()
-            load_v(w, d).wait()
+
+            @pl.when(jnp.logical_not(late))
+            def _():
+                load_held(w, d).wait()
+                load_m(w, d).wait()
+                load_v(w, d).wait()
+
         for d in range(2):
             so_far = slot_of(w, d, n - 2)
 
@@ -165,28 +180,27 @@
     for w, d in units:
         forward(w, d, n - 3)
     for w, d in units:
-        if w < 2:
+        if w == 2:
             forward(w, d, n - 2)
         else:
             pass_new(w, d, n - 3).wait()
-    for w, d in units:
-        if w < 2:
-            pass_new(w, d, n - 2).wait()
+    for d in range(2):
+        pass_new(2, d, n - 2).wait()
 
 
 def put_out(n, *refs):
     arrays, last, results, sem, block_sem = refs[:9], refs[9:11], refs[11:20], refs[20], refs[21]
     me = lax.axis_index("dp")
-    rows = last[0].shape[0]
+    rows = last[0].shape[1]
     copies = []
     for i, (a, r) in enumerate(zip(arrays, results, strict=True)):
         for d in range(2):
-            if i == 2:
+            if i < 2:
                 for hops in range(n - 1):
                     owner = lax.rem(me + (n - hops if d == 0 else hops), n)
                     piece = pl.ds(pl.multiple_of(owner * rows, rows), rows)
-                    source = last[d] if hops == n - 2 else a.at[d, piece]
-                    copies.append(pltpu.make_async_copy(source, r.at[d, piece], block_sem.at[d, hops]))
+                    source = last[d].at[i] if hops == n - 2 else a.at[d, piece]
+                    copies.append(pltpu.make_async_copy(source, r.at[d, piece], block_sem.at[i, d, hops]))
             else:
                 copies.append(pltpu.make_async_copy(a.at[d], r.at[d], sem.at[i, d]))
     for one in copies:
@@ -195,13 +209,14 @@
         one.wait()
 
 
-def put_last(n, so_far, from_left, from_right, result, sem):
+def put_last(n, gate, up, from_left, from_right, new_gate, new_up, sem):
     me = lax.axis_index("dp")
-    rows = from_left.shape[0]
+    rows = from_left.shape[1]
     copies = []
     for d, one in enumerate((from_left, from_right)):
         owner = lax.rem(me + (1 if d == 0 else n - 1), n)
-        copies.append(pltpu.make_async_copy(one, result.at[d, pl.ds(pl.multiple_of(owner * rows, rows), rows)], sem.at[d]))
+        for i, result in enumerate((new_gate, new_up)):
+            copies.append(pltpu.make_async_copy(one.at[i], result.at[d, pl.ds(pl.multiple_of(owner * rows, rows), rows)], sem.at[i, d]))
     for one in copies:
         one.start()
     for one in copies:
@@ -219,7 +234,7 @@
         inputs = (pltpu.with_memory_space_constraint(x, pltpu.HBM) for x in (*terms, *weights, *m, *v))
         made = pl.pallas_call(
             functools.partial(kernel, n),
-            out_shape=(*(pltpu.VMEM(x.shape, x.dtype) for x in (*weights, *m, *v)), *(pltpu.VMEM(shard[2][1:], BF16),) * 2),
+            out_shape=(*(pltpu.VMEM(x.shape, x.dtype) for x in (*weights, *m, *v)), *(pltpu.VMEM((2, *shard[0][1:]), BF16),) * 2),
             in_specs=[hbm] * 12,
             out_specs=(vmem,) * 11,
             scratch_shapes=[
@@ -236,7 +251,7 @@
                 dma((3, 2)),
                 pltpu.SemaphoreType.REGULAR((3, 2)),
             ],
-            compiler_params=pltpu.CompilerParams(collective_id=0, has_side_effects=True, vmem_limit_bytes=20 * 2**20),
+            compiler_params=pltpu.CompilerParams(collective_id=0, has_side_effects=True, vmem_limit_bytes=ROOM),
             name="step",
         )(*inputs)
         last_0, last_1 = made[9:]
@@ -246,22 +261,22 @@
             out_shape=tuple(jax.ShapeDtypeStruct(x.shape, x.dtype) for x in (*weights, *m, *v)),
             in_specs=[vmem] * 11,
             out_specs=(hbm,) * 9,
-            scratch_shapes=[dma((9, 2)), dma((2, n - 1))],
-            compiler_params=pltpu.CompilerParams(has_side_effects=True, vmem_limit_bytes=20 * 2**20),
+            scratch_shapes=[dma((9, 2)), dma((2, 2, n - 1))],
+            compiler_params=pltpu.CompilerParams(has_side_effects=True, vmem_limit_bytes=ROOM),
             cost_estimate=pl.CostEstimate(flops=COST, bytes_accessed=80_000_000, transcendentals=0),
             name="put_out",
         )(*(pltpu.with_memory_space_constraint(x, pltpu.VMEM) for x in made))
-        down = pl.pallas_call(
+        first = pl.pallas_call(
             functools.partial(put_last, n),
-            out_shape=jax.ShapeDtypeStruct(weights[2].shape, BF16),
-            in_specs=[hbm, vmem, vmem],
-            out_specs=hbm,
-            input_output_aliases={0: 0},
-            scratch_shapes=[dma((2,))],
-            compiler_params=pltpu.CompilerParams(has_side_effects=True, vmem_limit_bytes=20 * 2**20),
+            out_shape=tuple(jax.ShapeDtypeStruct(x.shape, x.dtype) for x in weights[:2]),
+            in_specs=[hbm, hbm, vmem, vmem],
+            out_specs=(hbm, hbm),
+            input_output_aliases={0: 0, 1: 1},
+            scratch_shapes=[dma((2, 2))],
+            compiler_params=pltpu.CompilerParams(has_side_effects=True, vmem_limit_bytes=ROOM),
             name="put_last",
-        )(pltpu.with_memory_space_constraint(out[2], pltpu.HBM), *(pltpu.with_memory_space_constraint(x, pltpu.VMEM) for x in last))
-        return (*out[:2], down, *out[3:])
+        )(*(pltpu.with_memory_space_constraint(x, pltpu.HBM) for x in out[:2]), *(pltpu.with_memory_space_constraint(x, pltpu.VMEM) for x in last))
+        return (*first, *out[2:])
 
     all_of, cut = P(None, None, None), P(None, "dp", None)
     return jax.shard_map(

time: 532 us -> 527 us (level)
  Pallas kernels: 528 us -> 518 us
    pallas_call x1, Pallas kernels: 513 us -> 504 us  [step(): pl.pallas_call(functools.partial(kernel, n), out_shape=(*(pltpu.VMEM(x.sh...]
  transfers between devices with their start and end apart: 2 -> 2, of which waited for: 0 -> 1; matrix products, arithmetic and copies ran while one was open for 0% -> 0% of each run, Pallas kernels for 2% -> 2%
where the time goes in v3:
time: 527 us
  Pallas kernels  518 us (98%)
    pallas_call x1, Pallas kernels, step(): pl.pallas_call(functools.partial(kernel, n), out_shape=(*(pltpu.VMEM(x.sh...  504 us
    pallas_call x1, Pallas kernels, step(): pl.pallas_call(functools.partial(put_out, n), out_shape=tuple((jax.ShapeD...  12.9 us
  transfers between devices with their start and end apart: 2, of which 1 were waited for; matrix products, arithmetic and copies ran while one was open for 0% of the time, Pallas kernels for 2%

profile of v3, /device:TPU:22, one launch (start us, length us, event | category | flops | bytes accessed | tf_op | source)
XLA Modules:
  0.0 526.9 jit_solution(13376474895108357588)
XLA Ops:
  0.6 503.5 %step.1 = (bf16[2,896,2560]{2,1,0:T(8,128)(2,1)S(1)}, bf16[2,896,2560]{2,1,0:T(8,128)(2,1)S(1)}, bf16[2,2560,896]{2,1,0:T(8,128)(2,1)S(1)}, f32[2,112,2560]{2,1,...) custom-call(bf16[1,2,896,2560]{3,2,1,0:T(8,128)(2,1)} %refs_0_.1, ...), custom_call_target="tpu_custom_call" | custom-call | tf_op jit(solution)/shard_map/step/pallas_call | solution.py:235
  504.2 2.2 collective-permute-start
  506.4 1.1 collective-permute-start.1
  507.5 12.9 %put_out.1 = (bf16[2,896,2560]{2,1,0:T(8,128)(2,1)}, bf16[2,896,2560]{2,1,0:T(8,128)(2,1)}, bf16[2,2560,896]{2,1,0:T(8,128)(2,1)}, f32[2,112,2560]{2,1,0:T(8,128...) custom-call(bf16[2,896,2560]{2,1,0:T(8,128)(2,1)S(1)} %get-tuple-ele, ...), custom_call_target="tpu_custom_call" | custom-call | flops 100000000 | bytes 80000000 | tf_op jit(solution)/shard_map/put_out/pallas_call | solution.py:259
  520.4 5.0 collective-permute-done.from_left
  525.4 0.0 collective-permute-done.1.from_right
  525.4 1.4 put_last.1
Async XLA Ops:
  504.2 21.3 %collective-permute-start = (bf16[2,112,2560]{2,1,0:T(8,128)(2,1)S(1)}, bf16[2,112,2560]{2,1,0:T(8,128)(2,1)S(1)}, u32[]{:S(2)}, u32[]{:S(2)}) collective-permute-start(bf16[2,112,2560]{2,1,0:T(8,128)(2,1)S(1)} %get-tuple-element.40.refs_9_), channel_id=1, source_target_pairs={{0,1},{1,2},{2,3},{3,4},{4,5},{5,6},{6,7},{7,0},{8,9},{9,10},{10,1... | collective-permute-start | bytes 3440648 | tf_op jit(solution)/shard_map/ppermute | solution.py:258
  506.4 19.1 %collective-permute-start.1 = (bf16[2,112,2560]{2,1,0:T(8,128)(2,1)S(1)}, bf16[2,112,2560]{2,1,0:T(8,128)(2,1)S(1)}, u32[]{:S(2)}, u32[]{:S(2)}) collective-permute-start(bf16[2,112,2560]{2,1,0:T(8,128)(2,1)S(1)} %get-tuple-element.41.refs_10_), channel_id=1, source_target_pairs={{0,7},{1,0},{2,1},{3,2},{4,3},{5,4},{6,5},{7,6},{8,15},{9,8},{10,9... | collective-permute-start | bytes 3440648 | tf_op jit(solution)/shard_map/ppermute | solution.py:258

commit v4 on v3

--- a/solution.py
+++ b/solution.py
@@ -24,9 +24,9 @@
 def kernel(n, *refs):
     terms, weights, old_m, old_v = (refs[i : i + 3] for i in (0, 3, 6, 9))
     whole, new_m, new_v = (refs[i : i + 3] for i in (12, 15, 18))
-    last = refs[21:23]
-    slots, own, held = (refs[i : i + 3] for i in (23, 26, 29))
-    sum_send, sum_recv, out_send, out_recv, own_sem, held_sem, m_sem, v_sem, free = refs[32:]
+    last = (refs[21:23], refs[23:25])
+    slots, own, held = (refs[i : i + 3] for i in (25, 28, 31))
+    sum_send, sum_recv, out_send, out_recv, own_sem, held_sem, m_sem, v_sem, free = refs[34:]
     me = lax.axis_index("dp")
     right, left = lax.rem(me + 1, n), lax.rem(me + n - 1, n)
     ahead, behind, way = (right, left), (left, right), (1, -1)
@@ -65,7 +65,7 @@
 
     def pass_new(w, d, step):
         piece = whole[w].at[d, block(w, index(d, step))]
-        lands = last[d].at[w] if w < 2 and isinstance(step, int) and step == n - 3 else piece
+        lands = last[w][d] if w < 2 and isinstance(step, int) and step == n - 3 else piece
         return pltpu.make_async_remote_copy(
             src_ref=piece,
             dst_ref=lands,
@@ -86,21 +86,23 @@
             for c in range(0, whole[w].shape[2], across):
                 body(pl.ds(pl.multiple_of(i * high, high), high), pl.ds(c, across))
 
-    for w, d in units:
-        load_own(w, d, 2).start()
     barrier = pltpu.get_barrier_semaphore()
     for other in (left, right):
         pl.semaphore_signal(barrier, inc=1, device_id={"dp": other}, device_id_type=MESH)
     pl.semaphore_wait(barrier, 2)
 
     late = lax.rem(lax.axis_index("rep"), 2) == 0
-    for w, d in units:
-        load_held(w, d).start()
-        load_m(w, d).start()
-        load_v(w, d).start()
+
+    def load_rest():
+        for w, d in units:
+            load_own(w, d, 2).start()
+            load_held(w, d).start()
+            load_m(w, d).start()
+            load_v(w, d).start()
 
     @pl.when(late)
     def _():
+        load_rest()
         for w, d in units:
             load_held(w, d).wait()
             load_m(w, d).wait()
@@ -108,6 +110,7 @@
 
     for w, d in units:
         pass_sum(w, d, 0, terms[w].at[0, d, block(w, index(d, 1))]).start()
+    pl.when(jnp.logical_not(late))(load_rest)
 
     @pl.loop(1, n - 1)
     def _(step):
@@ -189,9 +192,9 @@
 
 
 def put_out(n, *refs):
-    arrays, last, results, sem, block_sem = refs[:9], refs[9:11], refs[11:20], refs[20], refs[21]
+    arrays, last, results, sem, block_sem = refs[:9], (refs[9:11], refs[11:13]), refs[13:22], refs[22], refs[23]
     me = lax.axis_index("dp")
-    rows = last[0].shape[1]
+    rows = last[0][0].shape[0]
     copies = []
     for i, (a, r) in enumerate(zip(arrays, results, strict=True)):
         for d in range(2):
@@ -199,7 +202,7 @@
                 for hops in range(n - 1):
                     owner = lax.rem(me + (n - hops if d == 0 else hops), n)
                     piece = pl.ds(pl.multiple_of(owner * rows, rows), rows)
-                    source = last[d].at[i] if hops == n - 2 else a.at[d, piece]
+                    source = last[i][d] if hops == n - 2 else a.at[d, piece]
                     copies.append(pltpu.make_async_copy(source, r.at[d, piece], block_sem.at[i, d, hops]))
             else:
                 copies.append(pltpu.make_async_copy(a.at[d], r.at[d], sem.at[i, d]))
@@ -209,14 +212,13 @@
         one.wait()
 
 
-def put_last(n, gate, up, from_left, from_right, new_gate, new_up, sem):
+def put_last(n, so_far, from_left, from_right, result, sem):
     me = lax.axis_index("dp")
-    rows = from_left.shape[1]
+    rows = from_left.shape[0]
     copies = []
     for d, one in enumerate((from_left, from_right)):
         owner = lax.rem(me + (1 if d == 0 else n - 1), n)
-        for i, result in enumerate((new_gate, new_up)):
-            copies.append(pltpu.make_async_copy(one.at[i], result.at[d, pl.ds(pl.multiple_of(owner * rows, rows), rows)], sem.at[i, d]))
+        copies.append(pltpu.make_async_copy(one, result.at[d, pl.ds(pl.multiple_of(owner * rows, rows), rows)], sem.at[d]))
     for one in copies:
         one.start()
     for one in copies:
@@ -234,9 +236,9 @@
         inputs = (pltpu.with_memory_space_constraint(x, pltpu.HBM) for x in (*terms, *weights, *m, *v))
         made = pl.pallas_call(
             functools.partial(kernel, n),
-            out_shape=(*(pltpu.VMEM(x.shape, x.dtype) for x in (*weights, *m, *v)), *(pltpu.VMEM((2, *shard[0][1:]), BF16),) * 2),
+            out_shape=(*(pltpu.VMEM(x.shape, x.dtype) for x in (*weights, *m, *v)), *(pltpu.VMEM(shard[0][1:], BF16),) * 4),
             in_specs=[hbm] * 12,
-            out_specs=(vmem,) * 11,
+            out_specs=(vmem,) * 13,
             scratch_shapes=[
                 *(pltpu.VMEM((2, SLOTS, *s[1:]), BF16) for s in shard),
                 *(pltpu.VMEM(s, BF16) for s in shard),
@@ -254,28 +256,31 @@
             compiler_params=pltpu.CompilerParams(collective_id=0, has_side_effects=True, vmem_limit_bytes=ROOM),
             name="step",
         )(*inputs)
-        last_0, last_1 = made[9:]
-        last = [lax.ppermute(one, "dp", [(i, (i + way) % n) for i in range(n)]) for one, way in ((last_0, 1), (last_1, -1))]
+        rings = [[(i, (i + way) % n) for i in range(n)] for way in (1, -1)]
+        last = [[lax.ppermute(made[9 + 2 * w + d], "dp", rings[d]) for d in range(2)] for w in range(2)]
         out = pl.pallas_call(
             functools.partial(put_out, n),
             out_shape=tuple(jax.ShapeDtypeStruct(x.shape, x.dtype) for x in (*weights, *m, *v)),
-            in_specs=[vmem] * 11,
+            in_specs=[vmem] * 13,
             out_specs=(hbm,) * 9,
             scratch_shapes=[dma((9, 2)), dma((2, 2, n - 1))],
             compiler_params=pltpu.CompilerParams(has_side_effects=True, vmem_limit_bytes=ROOM),
             cost_estimate=pl.CostEstimate(flops=COST, bytes_accessed=80_000_000, transcendentals=0),
             name="put_out",
         )(*(pltpu.with_memory_space_constraint(x, pltpu.VMEM) for x in made))
-        first = pl.pallas_call(
-            functools.partial(put_last, n),
-            out_shape=tuple(jax.ShapeDtypeStruct(x.shape, x.dtype) for x in weights[:2]),
-            in_specs=[hbm, hbm, vmem, vmem],
-            out_specs=(hbm, hbm),
-            input_output_aliases={0: 0, 1: 1},
-            scratch_shapes=[dma((2, 2))],
-            compiler_params=pltpu.CompilerParams(has_side_effects=True, vmem_limit_bytes=ROOM),
-            name="put_last",
-        )(*(pltpu.with_memory_space_constraint(x, pltpu.HBM) for x in out[:2]), *(pltpu.with_memory_space_constraint(x, pltpu.VMEM) for x in last))
+        first = [
+            pl.pallas_call(
+                functools.partial(put_last, n),
+                out_shape=jax.ShapeDtypeStruct(weights[w].shape, BF16),
+                in_specs=[hbm, vmem, vmem],
+                out_specs=hbm,
+                input_output_aliases={0: 0},
+                scratch_shapes=[dma((2,))],
+                compiler_params=pltpu.CompilerParams(has_side_effects=True, vmem_limit_bytes=ROOM),
+                name="put_last",
+            )(pltpu.with_memory_space_constraint(out[w], pltpu.HBM), *(pltpu.with_memory_space_constraint(x, pltpu.VMEM) for x in last[w]))
+            for w in range(2)
+        ]
         return (*first, *out[2:])
 
     all_of, cut = P(None, None, None), P(None, "dp", None)

time: 527 us -> 527 us (level)
  transfers between devices with their start and end apart: 2 -> 4, of which waited for: 1 -> 1; matrix products, arithmetic and copies ran while one was open for 0% -> 0% of each run, Pallas kernels for 2% -> 3%
where the time goes in v4:
time: 527 us; the launch traced here: 526 us
  Pallas kernels  519 us (98%)
  starting transfers between devices  6.57 us (1%)
    pallas_call x1, Pallas kernels, step(): pl.pallas_call(functools.partial(kernel, n), out_shape=(*(pltpu.VMEM(x.sh...  504 us
    pallas_call x1, Pallas kernels, step(): pl.pallas_call(functools.partial(put_out, n), out_shape=tuple((jax.ShapeD...  12.9 us
  transfers between devices with their start and end apart: 4, of which 1 were waited for; matrix products, arithmetic and copies ran while one was open for 0% of the time, Pallas kernels for 3%

profile of v4, /device:TPU:22, one launch (start us, length us, event | category | flops | bytes accessed | tf_op | source)
XLA Modules:
  0.0 526.4 jit_solution(17116863828173952509)
XLA Ops:
  0.6 504.1 %step.1 = (bf16[2,896,2560]{2,1,0:T(8,128)(2,1)S(1)}, bf16[2,896,2560]{2,1,0:T(8,128)(2,1)S(1)}, bf16[2,2560,896]{2,1,0:T(8,128)(2,1)S(1)}, f32[2,112,2560]{2,1,...) custom-call(bf16[1,2,896,2560]{3,2,1,0:T(8,128)(2,1)} %refs_0_.1, ...), custom_call_target="tpu_custom_call" | custom-call | tf_op jit(solution)/shard_map/step/pallas_call | solution.py:237
  504.8 2.5 collective-permute-start
  507.3 0.8 collective-permute-start.1
  508.1 1.2 collective-permute-start.2
  509.3 2.0 collective-permute-start.3
  511.3 12.9 %put_out.1 = (bf16[2,896,2560]{2,1,0:T(8,128)(2,1)}, bf16[2,896,2560]{2,1,0:T(8,128)(2,1)}, bf16[2,2560,896]{2,1,0:T(8,128)(2,1)}, f32[2,112,2560]{2,1,0:T(8,128...) custom-call(bf16[2,896,2560]{2,1,0:T(8,128)(2,1)S(1)} %get-tuple-ele, ...), custom_call_target="tpu_custom_call" | custom-call | flops 100000000 | bytes 80000000 | tf_op jit(solution)/shard_map/put_out/pallas_call | solution.py:261
  524.3 0.0 collective-permute-done.from_left
  524.3 0.0 collective-permute-done.1.from_right
  524.3 1.0 put_last.2
  525.3 0.1 collective-permute-done.2.from_left
  525.4 0.0 collective-permute-done.3.from_right
  525.4 1.0 put_last.3
Async XLA Ops:
  504.8 19.5 %collective-permute-start = (bf16[112,2560]{1,0:T(8,128)(2,1)S(1)}, bf16[112,2560]{1,0:T(8,128)(2,1)S(1)}, u32[]{:S(2)}, u32[]{:S(2)}) collective-permute-start(bf16[112,2560]{1,0:T(8,128)(2,1)S(1)} %get-tuple-element.40.refs_9_), channel_id=1, source_target_pairs={{0,1},{1,2},{2,3},{3,4},{4,5},{5,6},{6,7},{7,0},{8,9},{9,10},{10,1... | collective-permute-start | bytes 1720328 | tf_op jit(solution)/shard_map/ppermute | solution.py:260
  507.3 17.0 %collective-permute-start.1 = (bf16[112,2560]{1,0:T(8,128)(2,1)S(1)}, bf16[112,2560]{1,0:T(8,128)(2,1)S(1)}, u32[]{:S(2)}, u32[]{:S(2)}) collective-permute-start(bf16[112,2560]{1,0:T(8,128)(2,1)S(1)} %get-tuple-element.41.refs_10_), channel_id=1, source_target_pairs={{0,7},{1,0},{2,1},{3,2},{4,3},{5,4},{6,5},{7,6},{8,15},{9,8},{10,9... | collective-permute-start | bytes 1720328 | tf_op jit(solution)/shard_map/ppermute | solution.py:260
  508.1 17.3 %collective-permute-start.2 = (bf16[112,2560]{1,0:T(8,128)(2,1)S(1)}, bf16[112,2560]{1,0:T(8,128)(2,1)S(1)}, u32[]{:S(2)}, u32[]{:S(2)}) collective-permute-start(bf16[112,2560]{1,0:T(8,128)(2,1)S(1)} %get-tuple-element.42.refs_11_), channel_id=1, source_target_pairs={{0,1},{1,2},{2,3},{3,4},{4,5},{5,6},{6,7},{7,0},{8,9},{9,10},{10,1... | collective-permute-start | bytes 1720328 | tf_op jit(solution)/shard_map/ppermute | solution.py:260
  509.3 16.1 %collective-permute-start.3 = (bf16[112,2560]{1,0:T(8,128)(2,1)S(1)}, bf16[112,2560]{1,0:T(8,128)(2,1)S(1)}, u32[]{:S(2)}, u32[]{:S(2)}) collective-permute-start(bf16[112,2560]{1,0:T(8,128)(2,1)S(1)} %get-tuple-element.43.refs_12_), channel_id=1, source_target_pairs={{0,7},{1,0},{2,1},{3,2},{4,3},{5,4},{6,5},{7,6},{8,15},{9,8},{10,9... | collective-permute-start | bytes 1720328 | tf_op jit(solution)/shard_map/ppermute | solution.py:260

commit v5 on v4

--- a/solution.py
+++ b/solution.py
@@ -9,6 +9,7 @@
 
 MESH = pl.DeviceIdType.MESH
 SLOTS = 3
+TAIL = 32
 COST = 100_000_000
 ROOM = 17 * 2**20
 F32, BF16 = jnp.float32, jnp.bfloat16
@@ -24,9 +25,9 @@
 def kernel(n, *refs):
     terms, weights, old_m, old_v = (refs[i : i + 3] for i in (0, 3, 6, 9))
     whole, new_m, new_v = (refs[i : i + 3] for i in (12, 15, 18))
-    last = (refs[21:23], refs[23:25])
+    most, rest = refs[21:23], refs[23:25]
     slots, own, held = (refs[i : i + 3] for i in (25, 28, 31))
-    sum_send, sum_recv, out_send, out_recv, own_sem, held_sem, m_sem, v_sem, free = refs[34:]
+    sum_send, sum_recv, out_send, out_recv, own_sem, held_sem, m_sem, v_sem, rest_send, rest_recv, free = refs[34:]
     me = lax.axis_index("dp")
     right, left = lax.rem(me + 1, n), lax.rem(me + n - 1, n)
     ahead, behind, way = (right, left), (left, right), (1, -1)
@@ -65,7 +66,11 @@
 
     def pass_new(w, d, step):
         piece = whole[w].at[d, block(w, index(d, step))]
-        lands = last[w][d] if w < 2 and isinstance(step, int) and step == n - 3 else piece
+        lands = piece
+        if isinstance(step, int) and step == n - 3 and w < 2:
+            first, count = (0, rows[0]) if w == 0 else (rows[0], rows[1] - TAIL)
+            piece = whole[w].at[d, pl.ds(pl.multiple_of(index(d, step) * rows[w], rows[w]), count)]
+            lands = most[d].at[pl.ds(first, count)]
         return pltpu.make_async_remote_copy(
             src_ref=piece,
             dst_ref=lands,
@@ -75,6 +80,17 @@
             device_id_type=MESH,
         )
 
+    def pass_rest(d):
+        first = pl.multiple_of(index(d, n - 3) * rows[1] + (rows[1] - TAIL), 16)
+        return pltpu.make_async_remote_copy(
+            src_ref=whole[1].at[d, pl.ds(first, TAIL)],
+            dst_ref=rest[d],
+            send_sem=rest_send.at[d],
+            recv_sem=rest_recv.at[d],
+            device_id={"dp": ahead[d]},
+            device_id_type=MESH,
+        )
+
     def slot_of(w, d, step):
         return slots[w].at[d, lax.rem(step, SLOTS)]
 
@@ -95,9 +111,10 @@
 
     def load_rest():
         for w, d in units:
-            load_own(w, d, 2).start()
             load_held(w, d).start()
             load_m(w, d).start()
+        for w, d in units:
+            load_own(w, d, 2).start()
             load_v(w, d).start()
 
     @pl.when(late)
@@ -106,7 +123,6 @@
         for w, d in units:
             load_held(w, d).wait()
             load_m(w, d).wait()
-            load_v(w, d).wait()
 
     for w, d in units:
         pass_sum(w, d, 0, terms[w].at[0, d, block(w, index(d, 1))]).start()
@@ -147,11 +163,12 @@
             pass_sum(w, d, n - 2, slot_of(w, d, n - 2)).wait_send()
             load_own(w, d, 0).wait()
 
+            load_v(w, d).wait()
+
             @pl.when(jnp.logical_not(late))
             def _():
                 load_held(w, d).wait()
                 load_m(w, d).wait()
-                load_v(w, d).wait()
 
         for d in range(2):
             so_far = slot_of(w, d, n - 2)
@@ -182,19 +199,23 @@
 
     for w, d in units:
         forward(w, d, n - 3)
+        if w == 1:
+            pass_rest(d).start()
     for w, d in units:
         if w == 2:
             forward(w, d, n - 2)
         else:
             pass_new(w, d, n - 3).wait()
     for d in range(2):
+        pass_rest(d).wait()
         pass_new(2, d, n - 2).wait()
 
 
 def put_out(n, *refs):
-    arrays, last, results, sem, block_sem = refs[:9], (refs[9:11], refs[11:13]), refs[13:22], refs[22], refs[23]
+    arrays, most, rest, results = refs[:9], refs[9:11], refs[11:13], refs[13:22]
+    sem, block_sem, rest_sem = refs[22:]
     me = lax.axis_index("dp")
-    rows = last[0][0].shape[0]
+    rows = arrays[0].shape[1] // n
     copies = []
     for i, (a, r) in enumerate(zip(arrays, results, strict=True)):
         for d in range(2):
@@ -202,27 +223,48 @@
                 for hops in range(n - 1):
                     owner = lax.rem(me + (n - hops if d == 0 else hops), n)
                     piece = pl.ds(pl.multiple_of(owner * rows, rows), rows)
-                    source = last[i][d] if hops == n - 2 else a.at[d, piece]
+                    source = a.at[d, piece]
+                    if hops == n - 2 and i == 0:
+                        source = most[d].at[pl.ds(0, rows)]
+                    elif hops == n - 2:
+                        piece = pl.ds(pl.multiple_of(owner * rows, rows), rows - TAIL)
+                        source = most[d].at[pl.ds(rows, rows - TAIL)]
+                        tail = pl.ds(pl.multiple_of(owner * rows + (rows - TAIL), 16), TAIL)
+                        copies.append(pltpu.make_async_copy(rest[d], r.at[d, tail], rest_sem.at[d]))
                     copies.append(pltpu.make_async_copy(source, r.at[d, piece], block_sem.at[i, d, hops]))
             else:
                 copies.append(pltpu.make_async_copy(a.at[d], r.at[d], sem.at[i, d]))
+    run(copies)
+
+
+def run(copies):
     for one in copies:
         one.start()
     for one in copies:
         one.wait()
 
 
-def put_last(n, so_far, from_left, from_right, result, sem):
+def put_most(n, gate, up, from_left, from_right, new_gate, new_up, sem):
     me = lax.axis_index("dp")
-    rows = from_left.shape[0]
+    rows = gate.shape[1] // n
     copies = []
     for d, one in enumerate((from_left, from_right)):
         owner = lax.rem(me + (1 if d == 0 else n - 1), n)
-        copies.append(pltpu.make_async_copy(one, result.at[d, pl.ds(pl.multiple_of(owner * rows, rows), rows)], sem.at[d]))
-    for one in copies:
-        one.start()
-    for one in copies:
-        one.wait()
+        for i, (result, first, count) in enumerate(((new_gate, 0, rows), (new_up, rows, rows - TAIL))):
+            piece = pl.ds(pl.multiple_of(owner * rows, rows), count)
+            copies.append(pltpu.make_async_copy(one.at[pl.ds(first, count)], result.at[d, piece], sem.at[i, d]))
+    run(copies)
+
+
+def put_rest(n, up, from_left, from_right, new_up, sem):
+    me = lax.axis_index("dp")
+    rows = up.shape[1] // n
+    copies = []
+    for d, one in enumerate((from_left, from_right)):
+        owner = lax.rem(me + (1 if d == 0 else n - 1), n)
+        piece = pl.ds(pl.multiple_of(owner * rows + (rows - TAIL), 16), TAIL)
+        copies.append(pltpu.make_async_copy(one, new_up.at[d, piece], sem.at[d]))
+    run(copies)
 
 
 def solution(mesh):
@@ -231,12 +273,13 @@
     def step(*arrays):
         terms, weights, m, v = (arrays[i : i + 3] for i in (0, 3, 6, 9))
         shard = [one.shape for one in m]
+        cols = shard[0][2]
         hbm, vmem = pl.BlockSpec(memory_space=pltpu.HBM), pl.BlockSpec(memory_space=pltpu.VMEM)
         dma = pltpu.SemaphoreType.DMA
         inputs = (pltpu.with_memory_space_constraint(x, pltpu.HBM) for x in (*terms, *weights, *m, *v))
         made = pl.pallas_call(
             functools.partial(kernel, n),
-            out_shape=(*(pltpu.VMEM(x.shape, x.dtype) for x in (*weights, *m, *v)), *(pltpu.VMEM(shard[0][1:], BF16),) * 4),
+            out_shape=(*(pltpu.VMEM(x.shape, x.dtype) for x in (*weights, *m, *v)), *(pltpu.VMEM((rows, cols), BF16) for rows in (2 * shard[0][1] - TAIL, TAIL) for _ in range(2))),
             in_specs=[hbm] * 12,
             out_specs=(vmem,) * 13,
             scratch_shapes=[
@@ -251,37 +294,47 @@
                 dma((3, 2)),
                 dma((3, 2)),
                 dma((3, 2)),
+                dma((2,)),
+                dma((2,)),
                 pltpu.SemaphoreType.REGULAR((3, 2)),
             ],
             compiler_params=pltpu.CompilerParams(collective_id=0, has_side_effects=True, vmem_limit_bytes=ROOM),
             name="step",
         )(*inputs)
         rings = [[(i, (i + way) % n) for i in range(n)] for way in (1, -1)]
-        last = [[lax.ppermute(made[9 + 2 * w + d], "dp", rings[d]) for d in range(2)] for w in range(2)]
+        most, rest = ([lax.ppermute(made[at + d], "dp", rings[d]) for d in range(2)] for at in (9, 11))
         out = pl.pallas_call(
             functools.partial(put_out, n),
             out_shape=tuple(jax.ShapeDtypeStruct(x.shape, x.dtype) for x in (*weights, *m, *v)),
             in_specs=[vmem] * 13,
             out_specs=(hbm,) * 9,
-            scratch_shapes=[dma((9, 2)), dma((2, 2, n - 1))],
+            scratch_shapes=[dma((9, 2)), dma((2, 2, n - 1)), dma((2,))],
             compiler_params=pltpu.CompilerParams(has_side_effects=True, vmem_limit_bytes=ROOM),
             cost_estimate=pl.CostEstimate(flops=COST, bytes_accessed=80_000_000, transcendentals=0),
             name="put_out",
         )(*(pltpu.with_memory_space_constraint(x, pltpu.VMEM) for x in made))
-        first = [
-            pl.pallas_call(
-                functools.partial(put_last, n),
-                out_shape=jax.ShapeDtypeStruct(weights[w].shape, BF16),
-                in_specs=[hbm, vmem, vmem],
-                out_specs=hbm,
-                input_output_aliases={0: 0},
-                scratch_shapes=[dma((2,))],
-                compiler_params=pltpu.CompilerParams(has_side_effects=True, vmem_limit_bytes=ROOM),
-                name="put_last",
-            )(pltpu.with_memory_space_constraint(out[w], pltpu.HBM), *(pltpu.with_memory_space_constraint(x, pltpu.VMEM) for x in last[w]))
-            for w in range(2)
-        ]
-        return (*first, *out[2:])
+        in_hbm, in_vmem = (functools.partial(pltpu.with_memory_space_constraint, memory_space=x) for x in (pltpu.HBM, pltpu.VMEM))
+        gate, up = pl.pallas_call(
+            functools.partial(put_most, n),
+            out_shape=tuple(jax.ShapeDtypeStruct(x.shape, BF16) for x in weights[:2]),
+            in_specs=[hbm, hbm, vmem, vmem],
+            out_specs=(hbm, hbm),
+            input_output_aliases={0: 0, 1: 1},
+            scratch_shapes=[dma((2, 2))],
+            compiler_params=pltpu.CompilerParams(has_side_effects=True, vmem_limit_bytes=ROOM),
+            name="put_most",
+        )(*map(in_hbm, out[:2]), *map(in_vmem, most))
+        up = pl.pallas_call(
+            functools.partial(put_rest, n),
+            out_shape=jax.ShapeDtypeStruct(weights[1].shape, BF16),
+            in_specs=[hbm, vmem, vmem],
+            out_specs=hbm,
+            input_output_aliases={0: 0},
+            scratch_shapes=[dma((2,))],
+            compiler_params=pltpu.CompilerParams(has_side_effects=True, vmem_limit_bytes=ROOM),
+            name="put_rest",
+        )(in_hbm(up), *map(in_vmem, rest))
+        return (gate, up, *out[2:])
 
     all_of, cut = P(None, None, None), P(None, "dp", None)
     return jax.shard_map(

time: 527 us -> 526 us (level)
  no operation moved by 1% of the time
where the time goes in v5:
time: 526 us
  Pallas kernels  519 us (99%)
  starting transfers between devices  6.57 us (1%)
    pallas_call x1, Pallas kernels, step(): pl.pallas_call(functools.partial(kernel, n), out_shape=(*(pltpu.VMEM(x.sh...  504 us
    pallas_call x1, Pallas kernels, step(): pl.pallas_call(functools.partial(put_out, n), out_shape=tuple((jax.ShapeD...  12.9 us
  transfers between devices with their start and end apart: 4, of which 1 were waited for; matrix products, arithmetic and copies ran while one was open for 0% of the time, Pallas kernels for 3%

profile of v5, /device:TPU:22, one launch (start us, length us, event | category | flops | bytes accessed | tf_op | source)
XLA Modules:
  0.0 526.2 jit_solution(14238537966772454137)
XLA Ops:
  0.6 503.6 %step.1 = (bf16[2,896,2560]{2,1,0:T(8,128)(2,1)S(1)}, bf16[2,896,2560]{2,1,0:T(8,128)(2,1)S(1)}, bf16[2,2560,896]{2,1,0:T(8,128)(2,1)S(1)}, f32[2,112,2560]{2,1,...) custom-call(bf16[1,2,896,2560]{3,2,1,0:T(8,128)(2,1)} %refs_0_.1, ...), custom_call_target="tpu_custom_call" | custom-call | tf_op jit(solution)/shard_map/step/pallas_call | solution.py:280
  504.3 2.5 collective-permute-start
  506.8 0.8 collective-permute-start.1
  507.6 1.2 collective-permute-start.2
  508.8 2.0 collective-permute-start.3
  510.9 12.9 %put_out.1 = (bf16[2,896,2560]{2,1,0:T(8,128)(2,1)}, bf16[2,896,2560]{2,1,0:T(8,128)(2,1)}, bf16[2,2560,896]{2,1,0:T(8,128)(2,1)}, f32[2,112,2560]{2,1,0:T(8,128...) custom-call(bf16[2,896,2560]{2,1,0:T(8,128)(2,1)S(1)} %get-tuple-ele, ...), custom_call_target="tpu_custom_call" | custom-call | flops 100000000 | bytes 80000000 | tf_op jit(solution)/shard_map/put_out/pallas_call | solution.py:306
  523.8 0.0 collective-permute-done.from_left
  523.8 0.0 collective-permute-done.1.from_right
  523.8 1.3 put_most.1
  525.1 0.3 collective-permute-done.2.from_left
  525.4 0.0 collective-permute-done.3.from_right
  525.4 0.7 put_rest.1
Async XLA Ops:
  504.3 19.5 %collective-permute-start = (bf16[192,2560]{1,0:T(8,128)(2,1)S(1)}, bf16[192,2560]{1,0:T(8,128)(2,1)S(1)}, u32[]{:S(2)}, u32[]{:S(2)}) collective-permute-start(bf16[192,2560]{1,0:T(8,128)(2,1)S(1)} %get-tuple-element.42.refs_9_), channel_id=1, source_target_pairs={{0,1},{1,2},{2,3},{3,4},{4,5},{5,6},{6,7},{7,0},{8,9},{9,10},{10,1... | collective-permute-start | bytes 2949128 | tf_op jit(solution)/shard_map/ppermute | solution.py:305
  506.8 17.0 %collective-permute-start.1 = (bf16[192,2560]{1,0:T(8,128)(2,1)S(1)}, bf16[192,2560]{1,0:T(8,128)(2,1)S(1)}, u32[]{:S(2)}, u32[]{:S(2)}) collective-permute-start(bf16[192,2560]{1,0:T(8,128)(2,1)S(1)} %get-tuple-element.43.refs_10_), channel_id=1, source_target_pairs={{0,7},{1,0},{2,1},{3,2},{4,3},{5,4},{6,5},{7,6},{8,15},{9,8},{10,9... | collective-permute-start | bytes 2949128 | tf_op jit(solution)/shard_map/ppermute | solution.py:305
  507.6 17.8 %collective-permute-start.2 = (bf16[32,2560]{1,0:T(8,128)(2,1)S(1)}, bf16[32,2560]{1,0:T(8,128)(2,1)S(1)}, u32[]{:S(2)}, u32[]{:S(2)}) collective-permute-start(bf16[32,2560]{1,0:T(8,128)(2,1)S(1)} %get-tuple-element.44.refs_11_), channel_id=1, source_target_pairs={{0,1},{1,2},{2,3},{3,4},{4,5},{5,6},{6,7},{7,0},{8,9},{9,10},{10,1... | collective-permute-start | bytes 491528 | tf_op jit(solution)/shard_map/ppermute | solution.py:305
  508.8 16.6 %collective-permute-start.3 = (bf16[32,2560]{1,0:T(8,128)(2,1)S(1)}, bf16[32,2560]{1,0:T(8,128)(2,1)S(1)}, u32[]{:S(2)}, u32[]{:S(2)}) collective-permute-start(bf16[32,2560]{1,0:T(8,128)(2,1)S(1)} %get-tuple-element.45.refs_12_), channel_id=1, source_target_pairs={{0,7},{1,0},{2,1},{3,2},{4,3},{5,4},{6,5},{7,6},{8,15},{9,8},{10,9... | collective-permute-start | bytes 491528 | tf_op jit(solution)/shard_map/ppermute | solution.py:305

commit v6 on v5

--- a/solution.py
+++ b/solution.py
@@ -27,7 +27,7 @@
     whole, new_m, new_v = (refs[i : i + 3] for i in (12, 15, 18))
     most, rest = refs[21:23], refs[23:25]
     slots, own, held = (refs[i : i + 3] for i in (25, 28, 31))
-    sum_send, sum_recv, out_send, out_recv, own_sem, held_sem, m_sem, v_sem, rest_send, rest_recv, free = refs[34:]
+    sum_send, sum_recv, out_send, out_recv, own_sem, held_sem, m_sem, v_sem, rest_send, rest_recv, here, free = refs[34:]
     me = lax.axis_index("dp")
     right, left = lax.rem(me + 1, n), lax.rem(me + n - 1, n)
     ahead, behind, way = (right, left), (left, right), (1, -1)
@@ -103,9 +103,9 @@
                 body(pl.ds(pl.multiple_of(i * high, high), high), pl.ds(c, across))
 
     barrier = pltpu.get_barrier_semaphore()
-    for other in (left, right):
-        pl.semaphore_signal(barrier, inc=1, device_id={"dp": other}, device_id_type=MESH)
-    pl.semaphore_wait(barrier, 2)
+    pl.semaphore_signal(barrier, inc=1, device_id={"dp": left}, device_id_type=MESH)
+    pl.semaphore_wait(barrier, 1)
+    pl.semaphore_signal(here, inc=1, device_id={"dp": right}, device_id_type=MESH)
 
     late = lax.rem(lax.axis_index("rep"), 2) == 0
 
@@ -124,9 +124,14 @@
             load_held(w, d).wait()
             load_m(w, d).wait()
 
-    for w, d in units:
-        pass_sum(w, d, 0, terms[w].at[0, d, block(w, index(d, 1))]).start()
+    def send_first(d):
+        for w in order:
+            pass_sum(w, d, 0, terms[w].at[0, d, block(w, index(d, 1))]).start()
+
+    send_first(0)
     pl.when(jnp.logical_not(late))(load_rest)
+    pl.semaphore_wait(here, 1)
+    send_first(1)
 
     @pl.loop(1, n - 1)
     def _(step):
@@ -296,6 +301,7 @@
                 dma((3, 2)),
                 dma((2,)),
                 dma((2,)),
+                pltpu.SemaphoreType.REGULAR,
                 pltpu.SemaphoreType.REGULAR((3, 2)),
             ],
             compiler_params=pltpu.CompilerParams(collective_id=0, has_side_effects=True, vmem_limit_bytes=ROOM),

time: 526 us -> 528 us (level)
  transfers between devices with their start and end apart: 4 -> 4, of which waited for: 1 -> 2; matrix products, arithmetic and copies ran while one was open for 0% -> 0% of each run, Pallas kernels for 3% -> 3%
where the time goes in v6:
time: 528 us
  Pallas kernels  516 us (98%)
  starting transfers between devices  6.56 us (1%)
  waiting for transfers between devices  5.46 us (1%)
    pallas_call x1, Pallas kernels, step(): pl.pallas_call(functools.partial(kernel, n), out_shape=(*(pltpu.VMEM(x.sh...  501 us
    pallas_call x1, Pallas kernels, step(): pl.pallas_call(functools.partial(put_out, n), out_shape=tuple((jax.ShapeD...  12.9 us
  transfers between devices with their start and end apart: 4, of which 2 were waited for; matrix products, arithmetic and copies ran while one was open for 0% of the time, Pallas kernels for 3%

profile of v6, /device:TPU:22, one launch (start us, length us, event | category | flops | bytes accessed | tf_op | source)
XLA Modules:
  0.0 528.3 jit_solution(4234847838571702880)
XLA Ops:
  0.6 500.7 %step.1 = (bf16[2,896,2560]{2,1,0:T(8,128)(2,1)S(1)}, bf16[2,896,2560]{2,1,0:T(8,128)(2,1)S(1)}, bf16[2,2560,896]{2,1,0:T(8,128)(2,1)S(1)}, f32[2,112,2560]{2,1,...) custom-call(bf16[1,2,896,2560]{3,2,1,0:T(8,128)(2,1)} %refs_0_.1, ...), custom_call_target="tpu_custom_call" | custom-call | tf_op jit(solution)/shard_map/step/pallas_call | solution.py:285
  501.3 0.1 collective-permute-start
  501.4 3.2 collective-permute-start.1
  504.6 0.0 collective-permute-start.2
  504.6 3.2 collective-permute-start.3
  507.9 12.9 %put_out.1 = (bf16[2,896,2560]{2,1,0:T(8,128)(2,1)}, bf16[2,896,2560]{2,1,0:T(8,128)(2,1)}, bf16[2,2560,896]{2,1,0:T(8,128)(2,1)}, f32[2,112,2560]{2,1,0:T(8,128...) custom-call(bf16[2,896,2560]{2,1,0:T(8,128)(2,1)S(1)} %get-tuple-ele, ...), custom_call_target="tpu_custom_call" | custom-call | flops 100000000 | bytes 80000000 | tf_op jit(solution)/shard_map/put_out/pallas_call | solution.py:312
  520.8 5.0 collective-permute-done.from_left
  525.8 0.0 collective-permute-done.1.from_right
  525.8 1.3 put_most.1
  527.1 0.4 collective-permute-done.2.from_left
  527.6 0.0 collective-permute-done.3.from_right
  527.6 0.7 put_rest.1
Async XLA Ops:
  501.3 24.5 %collective-permute-start = (bf16[192,2560]{1,0:T(8,128)(2,1)S(1)}, bf16[192,2560]{1,0:T(8,128)(2,1)S(1)}, u32[]{:S(2)}, u32[]{:S(2)}) collective-permute-start(bf16[192,2560]{1,0:T(8,128)(2,1)S(1)} %get-tuple-element.42.refs_9_), channel_id=1, source_target_pairs={{0,1},{1,2},{2,3},{3,4},{4,5},{5,6},{6,7},{7,0},{8,9},{9,10},{10,1... | collective-permute-start | bytes 2949128 | tf_op jit(solution)/shard_map/ppermute | solution.py:311
  501.4 24.4 %collective-permute-start.1 = (bf16[192,2560]{1,0:T(8,128)(2,1)S(1)}, bf16[192,2560]{1,0:T(8,128)(2,1)S(1)}, u32[]{:S(2)}, u32[]{:S(2)}) collective-permute-start(bf16[192,2560]{1,0:T(8,128)(2,1)S(1)} %get-tuple-element.43.refs_10_), channel_id=1, source_target_pairs={{0,7},{1,0},{2,1},{3,2},{4,3},{5,4},{6,5},{7,6},{8,15},{9,8},{10,9... | collective-permute-start | bytes 2949128 | tf_op jit(solution)/shard_map/ppermute | solution.py:311
  504.6 22.9 %collective-permute-start.2 = (bf16[32,2560]{1,0:T(8,128)(2,1)S(1)}, bf16[32,2560]{1,0:T(8,128)(2,1)S(1)}, u32[]{:S(2)}, u32[]{:S(2)}) collective-permute-start(bf16[32,2560]{1,0:T(8,128)(2,1)S(1)} %get-tuple-element.44.refs_11_), channel_id=1, source_target_pairs={{0,1},{1,2},{2,3},{3,4},{4,5},{5,6},{6,7},{7,0},{8,9},{9,10},{10,1... | collective-permute-start | bytes 491528 | tf_op jit(solution)/shard_map/ppermute | solution.py:311
  504.6 22.9 %collective-permute-start.3 = (bf16[32,2560]{1,0:T(8,128)(2,1)S(1)}, bf16[32,2560]{1,0:T(8,128)(2,1)S(1)}, u32[]{:S(2)}, u32[]{:S(2)}) collective-permute-start(bf16[32,2560]{1,0:T(8,128)(2,1)S(1)} %get-tuple-element.45.refs_12_), channel_id=1, source_target_pairs={{0,7},{1,0},{2,1},{3,2},{4,3},{5,4},{6,5},{7,6},{8,15},{9,8},{10,9... | collective-permute-start | bytes 491528 | tf_op jit(solution)/shard_map/ppermute | solution.py:311

commit v7 on v6

--- a/solution.py
+++ b/solution.py
@@ -123,6 +123,7 @@
         for w, d in units:
             load_held(w, d).wait()
             load_m(w, d).wait()
+            load_v(w, d).wait()
 
     def send_first(d):
         for w in order:
@@ -168,12 +169,12 @@
             pass_sum(w, d, n - 2, slot_of(w, d, n - 2)).wait_send()
             load_own(w, d, 0).wait()
 
-            load_v(w, d).wait()
 
             @pl.when(jnp.logical_not(late))
             def _():
                 load_held(w, d).wait()
                 load_m(w, d).wait()
+                load_v(w, d).wait()
 
         for d in range(2):
             so_far = slot_of(w, d, n - 2)

time: 528 us -> 528 us (level)
  no operation moved by 1% of the time
where the time goes in v7:
time: 528 us
  Pallas kernels  516 us (98%)
  starting transfers between devices  6.56 us (1%)
    pallas_call x1, Pallas kernels, step(): pl.pallas_call(functools.partial(kernel, n), out_shape=(*(pltpu.VMEM(x.sh...  501 us
    pallas_call x1, Pallas kernels, step(): pl.pallas_call(functools.partial(put_out, n), out_shape=tuple((jax.ShapeD...  12.9 us
  transfers between devices with their start and end apart: 4, of which 2 were waited for; matrix products, arithmetic and copies ran while one was open for 0% of the time, Pallas kernels for 3%

profile of v7, /device:TPU:22, one launch (start us, length us, event | category | flops | bytes accessed | tf_op | source)
XLA Modules:
  0.0 527.8 jit_solution(15252495874185249036)
XLA Ops:
  0.6 500.7 %step.1 = (bf16[2,896,2560]{2,1,0:T(8,128)(2,1)S(1)}, bf16[2,896,2560]{2,1,0:T(8,128)(2,1)S(1)}, bf16[2,2560,896]{2,1,0:T(8,128)(2,1)S(1)}, f32[2,112,2560]{2,1,...) custom-call(bf16[1,2,896,2560]{3,2,1,0:T(8,128)(2,1)} %refs_0_.1, ...), custom_call_target="tpu_custom_call" | custom-call | tf_op jit(solution)/shard_map/step/pallas_call | solution.py:286
  501.3 0.1 collective-permute-start
  501.4 3.2 collective-permute-start.1
  504.6 0.0 collective-permute-start.2
  504.6 3.2 collective-permute-start.3
  507.9 12.9 %put_out.1 = (bf16[2,896,2560]{2,1,0:T(8,128)(2,1)}, bf16[2,896,2560]{2,1,0:T(8,128)(2,1)}, bf16[2,2560,896]{2,1,0:T(8,128)(2,1)}, f32[2,112,2560]{2,1,0:T(8,128...) custom-call(bf16[2,896,2560]{2,1,0:T(8,128)(2,1)S(1)} %get-tuple-ele, ...), custom_call_target="tpu_custom_call" | custom-call | flops 100000000 | bytes 80000000 | tf_op jit(solution)/shard_map/put_out/pallas_call | solution.py:313
  520.8 4.5 collective-permute-done.from_left
  525.3 0.0 collective-permute-done.1.from_right
  525.3 1.3 put_most.1
  526.7 0.4 collective-permute-done.2.from_left
  527.1 0.0 collective-permute-done.3.from_right
  527.1 0.7 put_rest.1
Async XLA Ops:
  501.3 24.0 %collective-permute-start = (bf16[192,2560]{1,0:T(8,128)(2,1)S(1)}, bf16[192,2560]{1,0:T(8,128)(2,1)S(1)}, u32[]{:S(2)}, u32[]{:S(2)}) collective-permute-start(bf16[192,2560]{1,0:T(8,128)(2,1)S(1)} %get-tuple-element.42.refs_9_), channel_id=1, source_target_pairs={{0,1},{1,2},{2,3},{3,4},{4,5},{5,6},{6,7},{7,0},{8,9},{9,10},{10,1... | collective-permute-start | bytes 2949128 | tf_op jit(solution)/shard_map/ppermute | solution.py:312
  501.4 23.9 %collective-permute-start.1 = (bf16[192,2560]{1,0:T(8,128)(2,1)S(1)}, bf16[192,2560]{1,0:T(8,128)(2,1)S(1)}, u32[]{:S(2)}, u32[]{:S(2)}) collective-permute-start(bf16[192,2560]{1,0:T(8,128)(2,1)S(1)} %get-tuple-element.43.refs_10_), channel_id=1, source_target_pairs={{0,7},{1,0},{2,1},{3,2},{4,3},{5,4},{6,5},{7,6},{8,15},{9,8},{10,9... | collective-permute-start | bytes 2949128 | tf_op jit(solution)/shard_map/ppermute | solution.py:312
  504.6 22.5 %collective-permute-start.2 = (bf16[32,2560]{1,0:T(8,128)(2,1)S(1)}, bf16[32,2560]{1,0:T(8,128)(2,1)S(1)}, u32[]{:S(2)}, u32[]{:S(2)}) collective-permute-start(bf16[32,2560]{1,0:T(8,128)(2,1)S(1)} %get-tuple-element.44.refs_11_), channel_id=1, source_target_pairs={{0,1},{1,2},{2,3},{3,4},{4,5},{5,6},{6,7},{7,0},{8,9},{9,10},{10,1... | collective-permute-start | bytes 491528 | tf_op jit(solution)/shard_map/ppermute | solution.py:312
  504.6 22.5 %collective-permute-start.3 = (bf16[32,2560]{1,0:T(8,128)(2,1)S(1)}, bf16[32,2560]{1,0:T(8,128)(2,1)S(1)}, u32[]{:S(2)}, u32[]{:S(2)}) collective-permute-start(bf16[32,2560]{1,0:T(8,128)(2,1)S(1)} %get-tuple-element.45.refs_12_), channel_id=1, source_target_pairs={{0,7},{1,0},{2,1},{3,2},{4,3},{5,4},{6,5},{7,6},{8,15},{9,8},{10,9... | collective-permute-start | bytes 491528 | tf_op jit(solution)/shard_map/ppermute | solution.py:312

commit v8 on v5

--- a/solution.py
+++ b/solution.py
@@ -109,24 +109,23 @@
 
     late = lax.rem(lax.axis_index("rep"), 2) == 0
 
-    def load_rest():
-        for w, d in units:
-            load_held(w, d).start()
-            load_m(w, d).start()
-        for w, d in units:
-            load_own(w, d, 2).start()
-            load_v(w, d).start()
+    def load_state(w, d):
+        load_held(w, d).start()
+        load_m(w, d).start()
+        load_v(w, d).start()
 
     @pl.when(late)
     def _():
-        load_rest()
+        for w, d in units:
+            load_state(w, d)
         for w, d in units:
             load_held(w, d).wait()
             load_m(w, d).wait()
 
     for w, d in units:
         pass_sum(w, d, 0, terms[w].at[0, d, block(w, index(d, 1))]).start()
-    pl.when(jnp.logical_not(late))(load_rest)
+    for w, d in units:
+        load_own(w, d, 2).start()
 
     @pl.loop(1, n - 1)
     def _(step):
@@ -149,6 +148,7 @@
                 over(w, 1280, add)
             for d in range(2):
                 load_own(w, d, step + 2).start()
+                pl.when((step == 1) & jnp.logical_not(late))(functools.partial(load_state, w, d))
 
                 @pl.when(step >= SLOTS)
                 def _():

time: 526 us -> 526 us (level)
  transfers between devices with their start and end apart: 4 -> 4, of which waited for: 1 -> 2; matrix products, arithmetic and copies ran while one was open for 0% -> 0% of each run, Pallas kernels for 3% -> 3%
where the time goes in v8:
time: 526 us
  Pallas kernels  518 us (98%)
  starting transfers between devices  6.57 us (1%)
    pallas_call x1, Pallas kernels, step(): pl.pallas_call(functools.partial(kernel, n), out_shape=(*(pltpu.VMEM(x.sh...  503 us
    pallas_call x1, Pallas kernels, step(): pl.pallas_call(functools.partial(put_out, n), out_shape=tuple((jax.ShapeD...  12.9 us
  transfers between devices with their start and end apart: 4, of which 2 were waited for; matrix products, arithmetic and copies ran while one was open for 0% of the time, Pallas kernels for 3%

profile of v8, /device:TPU:22, one launch (start us, length us, event | category | flops | bytes accessed | tf_op | source)
XLA Modules:
  0.0 526.2 jit_solution(11626953169422383960)
XLA Ops:
  0.6 502.8 %step.1 = (bf16[2,896,2560]{2,1,0:T(8,128)(2,1)S(1)}, bf16[2,896,2560]{2,1,0:T(8,128)(2,1)S(1)}, bf16[2,2560,896]{2,1,0:T(8,128)(2,1)S(1)}, f32[2,112,2560]{2,1,...) custom-call(bf16[1,2,896,2560]{3,2,1,0:T(8,128)(2,1)} %refs_0_.1, ...), custom_call_target="tpu_custom_call" | custom-call | tf_op jit(solution)/shard_map/step/pallas_call | solution.py:280
  503.5 2.5 collective-permute-start
  506.0 0.8 collective-permute-start.1
  506.8 1.2 collective-permute-start.2
  508.0 2.0 collective-permute-start.3
  510.0 12.9 %put_out.1 = (bf16[2,896,2560]{2,1,0:T(8,128)(2,1)}, bf16[2,896,2560]{2,1,0:T(8,128)(2,1)}, bf16[2,2560,896]{2,1,0:T(8,128)(2,1)}, f32[2,112,2560]{2,1,0:T(8,128...) custom-call(bf16[2,896,2560]{2,1,0:T(8,128)(2,1)S(1)} %get-tuple-ele, ...), custom_call_target="tpu_custom_call" | custom-call | flops 100000000 | bytes 80000000 | tf_op jit(solution)/shard_map/put_out/pallas_call | solution.py:306
  523.0 0.7 collective-permute-done.from_left
  523.7 0.0 collective-permute-done.1.from_right
  523.7 1.3 put_most.1
  525.0 0.4 collective-permute-done.2.from_left
  525.4 0.0 collective-permute-done.3.from_right
  525.4 0.7 put_rest.1
Async XLA Ops:
  503.5 20.2 %collective-permute-start = (bf16[192,2560]{1,0:T(8,128)(2,1)S(1)}, bf16[192,2560]{1,0:T(8,128)(2,1)S(1)}, u32[]{:S(2)}, u32[]{:S(2)}) collective-permute-start(bf16[192,2560]{1,0:T(8,128)(2,1)S(1)} %get-tuple-element.42.refs_9_), channel_id=1, source_target_pairs={{0,1},{1,2},{2,3},{3,4},{4,5},{5,6},{6,7},{7,0},{8,9},{9,10},{10,1... | collective-permute-start | bytes 2949128 | tf_op jit(solution)/shard_map/ppermute | solution.py:305
  506.0 17.7 %collective-permute-start.1 = (bf16[192,2560]{1,0:T(8,128)(2,1)S(1)}, bf16[192,2560]{1,0:T(8,128)(2,1)S(1)}, u32[]{:S(2)}, u32[]{:S(2)}) collective-permute-start(bf16[192,2560]{1,0:T(8,128)(2,1)S(1)} %get-tuple-element.43.refs_10_), channel_id=1, source_target_pairs={{0,7},{1,0},{2,1},{3,2},{4,3},{5,4},{6,5},{7,6},{8,15},{9,8},{10,9... | collective-permute-start | bytes 2949128 | tf_op jit(solution)/shard_map/ppermute | solution.py:305
  506.8 18.6 %collective-permute-start.2 = (bf16[32,2560]{1,0:T(8,128)(2,1)S(1)}, bf16[32,2560]{1,0:T(8,128)(2,1)S(1)}, u32[]{:S(2)}, u32[]{:S(2)}) collective-permute-start(bf16[32,2560]{1,0:T(8,128)(2,1)S(1)} %get-tuple-element.44.refs_11_), channel_id=1, source_target_pairs={{0,1},{1,2},{2,3},{3,4},{4,5},{5,6},{6,7},{7,0},{8,9},{9,10},{10,1... | collective-permute-start | bytes 491528 | tf_op jit(solution)/shard_map/ppermute | solution.py:305
  508.0 17.4 %collective-permute-start.3 = (bf16[32,2560]{1,0:T(8,128)(2,1)S(1)}, bf16[32,2560]{1,0:T(8,128)(2,1)S(1)}, u32[]{:S(2)}, u32[]{:S(2)}) collective-permute-start(bf16[32,2560]{1,0:T(8,128)(2,1)S(1)} %get-tuple-element.45.refs_12_), channel_id=1, source_target_pairs={{0,7},{1,0},{2,1},{3,2},{4,3},{5,4},{6,5},{7,6},{8,15},{9,8},{10,9... | collective-permute-start | bytes 491528 | tf_op jit(solution)/shard_map/ppermute | solution.py:305
